TPU v7x, 32 devices: a whole 2x2x4 slice. The times are simulated.
32 devices in a mesh: groups: 2 (over y), rows: 16 (over z, x, core).
Axes of the slice: x: 2, y: 2, z: 4, core: 2. Of those that a mesh axis runs over, the one named last changes fastest.
Arguments:
- pair_repr: bfloat16 [256, 128, 128], P('groups', 'rows'), parts along dimension 0, may hold values from -6 to 6
- single_repr: bfloat16 [256, 384], P(('groups', 'rows')), parts along dimension 0, may hold values from -6 to 6
- residue_index: int32 [256], P('groups'), parts along dimension 0, may hold values from 0 to 47
- chain_index: int32 [256], P('groups'), parts along dimension 0, may hold values from 0 to 3
- complex_index: int32 [256], P('groups'), parts along dimension 0, may hold values from 0 to 7, never falling along the last dimension, each value on 1 to 96 neighbouring positions
- pad_mask: int32 [256], P('groups'), parts along dimension 0, may hold values 0 or 1
- w_query: bfloat16 [384, 384], replicated, may hold values from -3 to 3
- w_key: bfloat16 [384, 384], replicated, may hold values from -3.1 to 3.1
- w_value: bfloat16 [384, 384], replicated, may hold values from -0.3125 to 0.3125
- w_gate: bfloat16 [384, 384], replicated, may hold values from -0.3125 to 0.3125
- w_out: bfloat16 [384, 384], replicated, may hold values from -2.5 to 2.5
- w_bias: bfloat16 [128, 16], replicated, may hold values from -0.5 to 0.5
- rel_table: bfloat16 [66, 128], replicated, may hold values from -6 to 6
- w_mix_a: bfloat16 [384, 128], replicated, may hold values from -0.3125 to 0.3125
- w_mix_b: bfloat16 [384, 128], replicated, may hold values from -0.3125 to 0.3125
- w_hidden_a: bfloat16 [128, 512], replicated, may hold values from -0.5 to 0.5
- w_hidden_b: bfloat16 [128, 512], replicated, may hold values from -0.5 to 0.5
- w_hidden_out: bfloat16 [512, 128], replicated, may hold values from -0.25 to 0.25
- w_pae: bfloat16 [128, 64], replicated, may hold values from -30 to 30
- pae_bias: float32 [64], replicated, may hold values from -4 to 4
Outputs:
- refined: bfloat16 [256, 384], P(('groups', 'rows')), parts along dimension 0
- errors: float32 [256, 128], P(('groups', 'rows')), parts along dimension 0
There are 2 independent parts, one for each index of `groups`. A program takes and returns all parts, laid end to end along the dimension named above; an argument that names none is the same for every part. Nothing has to cross between parts.
Inputs may be any that keep to these rules, and one draw needn't show every extreme that they name: `complex_index`: never falls along the tokens; each complex holds 1 to 96 consecutive tokens.
All inputs are finite; a program needn't handle non-finite values.
Results may differ from a plain program's by a relative error of at most 0.023.
Values may be sent and summed in bfloat16 or wider, within the bound.
A program may use at most 128 MiB of HBM per device.

v0:
```python
import math
import jax
import jax.numpy as jnp
from jax import lax
from jax.sharding import PartitionSpec as P

epsilon = 1e-05
masked_score = -1e30


def norm_rows(values):
    center = values - jnp.mean(values, axis=-1, keepdims=True)
    spread = jnp.mean(center * center, axis=-1, keepdims=True)
    return center * lax.rsqrt(spread + epsilon)


def relative(res_query, chain_query, res_key, chain_key, rel_table):
    reach = (rel_table.shape[0] - 2) // 2
    offsets = jnp.clip(res_query[:, None] - res_key[None, :], -reach, reach) + reach
    bucket = jnp.where(chain_query[:, None] == chain_key[None, :], offsets, 2 * reach + 1)
    classes = jnp.arange(rel_table.shape[0], dtype=jnp.int32)
    onehot = (bucket[:, :, None] == classes[None, None, :]).astype(jnp.bfloat16)
    return jnp.einsum("qkr,rc->qkc", onehot, rel_table, preferred_element_type=jnp.float32)


def pair_tail(mixed, w_hidden_a, w_hidden_b, w_hidden_out, w_pae, pae_bias):
    width = mixed.shape[-1]
    flat = mixed.reshape(-1, width)
    normed = norm_rows(flat).astype(jnp.bfloat16)
    gate_part = jnp.dot(normed, w_hidden_a, preferred_element_type=jnp.float32)
    up_part = jnp.dot(normed, w_hidden_b, preferred_element_type=jnp.float32)
    hidden = (jax.nn.silu(gate_part) * up_part).astype(jnp.bfloat16)
    updated = flat + jnp.dot(hidden, w_hidden_out, preferred_element_type=jnp.float32)
    final = norm_rows(updated).astype(jnp.bfloat16)
    logits = jnp.dot(final, w_pae, preferred_element_type=jnp.float32) + pae_bias[None, :]
    probs = jax.nn.softmax(logits, axis=-1)
    bins = w_pae.shape[1]
    centers = (jnp.arange(bins, dtype=jnp.float32) + 0.5) * (32.0 / bins)
    return jnp.sum(probs * centers[None, :], axis=-1).reshape(mixed.shape[:-1])


def on_device(
    pair_repr,
    single_repr,
    residue_index,
    chain_index,
    complex_index,
    pad_mask,
    w_query,
    w_key,
    w_value,
    w_gate,
    w_out,
    w_bias,
    rel_table,
    w_mix_a,
    w_mix_b,
    w_hidden_a,
    w_hidden_b,
    w_hidden_out,
    w_pae,
    pae_bias,
):
    local_rows = single_repr.shape[0]
    head_count = w_bias.shape[1]
    head_size = single_repr.shape[1] // head_count
    first_row = lax.axis_index("rows") * local_rows
    row_ids = first_row + jnp.arange(local_rows, dtype=jnp.int32)
    res_local = lax.dynamic_slice_in_dim(residue_index, first_row, local_rows, 0)
    chain_local = lax.dynamic_slice_in_dim(chain_index, first_row, local_rows, 0)
    complex_local = lax.dynamic_slice_in_dim(complex_index, first_row, local_rows, 0)
    normed = norm_rows(single_repr.astype(jnp.float32)).astype(jnp.bfloat16)
    queries = jnp.dot(normed, w_query, preferred_element_type=jnp.float32).astype(jnp.bfloat16)
    keys_local = jnp.dot(normed, w_key, preferred_element_type=jnp.float32).astype(jnp.bfloat16)
    values_local = jnp.dot(normed, w_value, preferred_element_type=jnp.float32).astype(jnp.bfloat16)
    gating = jax.nn.sigmoid(jnp.dot(normed, w_gate, preferred_element_type=jnp.float32))
    pair_local = lax.all_to_all(pair_repr, "rows", split_axis=0, concat_axis=1, tiled=True)
    pair_in = pair_local.astype(jnp.float32) + relative(
        res_local, chain_local, residue_index, chain_index, rel_table
    )
    pair_bias = jnp.einsum(
        "qkc,ch->hqk",
        norm_rows(pair_in).astype(jnp.bfloat16),
        w_bias,
        preferred_element_type=jnp.float32,
    ).astype(jnp.bfloat16)
    query_heads = queries.reshape(local_rows, head_count, head_size)
    row_max = jnp.full((head_count, local_rows), masked_score, jnp.float32)
    key_part = lax.all_gather(keys_local, "rows", axis=0, tiled=True)
    value_part = lax.all_gather(values_local, "rows", axis=0, tiled=True)
    count = key_part.shape[0]
    key_heads = key_part.reshape(count, head_count, head_size)
    value_heads = value_part.reshape(count, head_count, head_size)
    scores = jnp.einsum(
        "qhd,khd->hqk", query_heads, key_heads, preferred_element_type=jnp.float32
    ) / math.sqrt(head_size)
    scores = scores + pair_bias.astype(jnp.float32)
    key_ids = jnp.arange(count, dtype=jnp.int32)
    allowed = (complex_local[:, None] == complex_index[None, :]) & (
        (pad_mask[None, :] == 1) | (row_ids[:, None] == key_ids[None, :])
    )
    scores = jnp.where(allowed[None], scores, masked_score)
    new_max = jnp.maximum(row_max, jnp.max(scores, axis=-1))
    expo = jnp.exp(scores - new_max[..., None])
    new_sum = jnp.sum(expo, axis=-1)
    added = jnp.einsum(
        "hqk,khd->hqd", expo.astype(jnp.bfloat16), value_heads, preferred_element_type=jnp.float32
    )
    attended = (
        (added / new_sum[..., None]).transpose(1, 0, 2).reshape(local_rows, head_count * head_size)
    )
    refined = (
        single_repr.astype(jnp.float32)
        + jnp.dot(
            (gating * attended).astype(jnp.bfloat16), w_out, preferred_element_type=jnp.float32
        )
    ).astype(jnp.bfloat16)
    renormed = norm_rows(refined.astype(jnp.float32)).astype(jnp.bfloat16)
    factor_a = jnp.dot(renormed, w_mix_a, preferred_element_type=jnp.float32).astype(jnp.bfloat16)
    factor_b = jnp.dot(renormed, w_mix_b, preferred_element_type=jnp.float32).astype(jnp.bfloat16)
    every_b = lax.all_gather(factor_b, "rows", axis=0, tiled=True)
    mixed = (
        pair_in + factor_a.astype(jnp.float32)[:, None, :] * every_b.astype(jnp.float32)[None, :, :]
    )
    errors = pair_tail(mixed, w_hidden_a, w_hidden_b, w_hidden_out, w_pae, pae_bias)
    return (refined, errors)


def solution(mesh):
    placed = (
        P("groups", "rows", None),
        P(("groups", "rows"), None),
        P("groups"),
        P("groups"),
        P("groups"),
        P("groups"),
        P(),
        P(),
        P(),
        P(),
        P(),
        P(),
        P(),
        P(),
        P(),
        P(),
        P(),
        P(),
        P(),
        P(),
    )
    return jax.shard_map(
        on_device,
        mesh=mesh,
        in_specs=placed,
        out_specs=(P(("groups", "rows"), None), P(("groups", "rows"), None)),
        check_vma=False,
    )
```

profile of v0, /device:TPU:0, one launch (start us, length us, event | category | flops | bytes accessed | tf_op | source)
XLA Modules:
  0.0 83.6 jit_solution(17553948313955501287)
XLA Ops:
  0.6 0.0 copy-start
  0.6 0.0 copy-start.7
  0.7 0.0 copy-start.8
  0.7 0.0 copy-start.9
  0.7 0.0 copy-start.3
  0.7 0.0 copy-start.6
  0.7 7.5 %all-to-all-start = ((bf16[128,8,128]{2,1,0:T(8,128)(2,1)}), bf16[128,8,128]{2,1,0:T(8,128)(2,1)S(1)}, u32[]{:S(2)}, u32[]{:S(2)}) async-start(bf16[128,8,128]{2,1,0:T(8,128)(2,1)} %param.20), calls=%async_computation | async-start | bytes 524288 | tf_op jit(solution)/shard_map/all_to_all | solution.py:77
  8.3 0.8 convert_reduce_fusion
  9.1 0.9 %fusion.30 = f32[8]{0:T(128)S(1)} fusion(bf16[8,384]{1,0:T(8,128)(2,1)} %param.21, f32[8]{0:T(128)S(1)} %broadcast_multiply_fusion.4), kind=kLoop, calls=%fused_computation.57 | loop fusion | flops 12280 | bytes 6208 | tf_op jit(solution)/shard_map/reduce_sum | solution.py:13
  10.0 1.2 %convolution_convert_fusion = bf16[8,384]{1,0:T(8,128)(2,1)S(1)} fusion(bf16[384,384]{1,0:T(8,128)(2,1)} %param.28, bf16[8,384]{1,0:T(8,128)(2,1)} %param.21, f32[8]{0:T(128)S(1)} %add_rsqrt_fusion.3, f32[8]{0:T(128)S(1)} %broadcast_multiply_fusion.4), kind=kOutput, calls=%fused_computation.18 | convolution fusion | flops 2374656 | bytes 307264 | tf_op jit(solution)/shard_map/dot_general | solution.py:75
  11.1 22.1 %all_gather.10 = bf16[128,384]{1,0:T(8,128)(2,1)S(1)} all-gather(bf16[8,384]{1,0:T(8,128)(2,1)S(1)} %convolution_convert_fusion), channel_id=1, replica_groups=mesh['groups'=2,'rows'=16] {'rows'}, dimensions={0}, use_global_device_ids=true | all-gather | bytes 104448 | tf_op jit(solution)/shard_map/all_gather | solution.py:90
  33.2 0.1 copy.32
  33.4 0.7 dynamic_slice.11
  34.1 0.7 dynamic_slice.10
  34.8 1.2 %convolution_convert_fusion.1 = bf16[8,384]{1,0:T(8,128)(2,1)S(1)} fusion(bf16[384,384]{1,0:T(8,128)(2,1)} %param.27, bf16[8,384]{1,0:T(8,128)(2,1)} %param.21, f32[8]{0:T(128)S(1)} %add_rsqrt_fusion.3, f32[8]{0:T(128)S(1)} %broadcast_multiply_fusion.4), kind=kOutput, calls=%fused_computation.19 | convolution fusion | flops 2374656 | bytes 307264 | tf_op jit(solution)/shard_map/dot_general | solution.py:74
  36.0 1.2 %convolution_convert_fusion.2 = bf16[8,384]{1,0:T(8,128)(2,1)S(1)} fusion(bf16[384,384]{1,0:T(8,128)(2,1)} %param.26, bf16[8,384]{1,0:T(8,128)(2,1)} %param.21, f32[8]{0:T(128)S(1)} %add_rsqrt_fusion.3, f32[8]{0:T(128)S(1)} %broadcast_multiply_fusion.4), kind=kOutput, calls=%fused_computation.20 | convolution fusion | flops 2374656 | bytes 307264 | tf_op jit(solution)/shard_map/dot_general | solution.py:73
  37.2 0.7 broadcast_compare_fusion
  37.9 17.7 %all_gather.9 = bf16[128,384]{1,0:T(8,128)(2,1)S(1)} all-gather(bf16[8,384]{1,0:T(8,128)(2,1)S(1)} %convolution_convert_fusion.1), channel_id=1, replica_groups=mesh['groups'=2,'rows'=16] {'rows'}, dimensions={0}, use_global_device_ids=true | all-gather | bytes 104448 | tf_op jit(solution)/shard_map/all_gather | solution.py:89
  55.6 0.1 copy.28
  55.7 0.1 reshape.245
  55.8 0.0 copy-done.9
  55.9 0.1 dynamic_slice.9
  55.9 0.1 fusion.37
  56.0 0.0 copy-done.7
  56.0 0.0 copy-done.8
  56.0 0.1 add_select_fusion
  56.1 0.0 all-to-all-done
  56.1 0.0 copy-done.3
  56.1 0.4 fusion.49
  56.6 0.4 multiply_reduce_fusion.2
  56.9 0.0 copy-done.6
  57.0 0.5 fusion.13
  57.4 0.2 fusion.50
  57.7 0.2 fusion.20
  57.8 0.2 fusion.2
  58.1 0.1 reshape.248
  58.2 0.0 copy-done
  58.2 0.0 copy-done.2
  58.2 0.0 copy-done.11
  58.2 0.5 convert_reduce_fusion.1
  58.7 0.0 copy-start.5
  58.7 0.0 copy-start.1
  58.7 0.2 fusion.32
  58.9 0.0 copy-done.14
  58.9 0.2 convolution_convert_fusion.3
  59.1 18.8 %all_gather.11 = bf16[128,128]{1,0:T(8,128)(2,1)S(1)} all-gather(bf16[8,128]{1,0:T(8,128)(2,1)S(1)} %convolution_convert_fusion.3), channel_id=1, replica_groups=mesh['groups'=2,'rows'=16] {'rows'}, dimensions={0}, use_global_device_ids=true | all-gather | bytes 34816 | tf_op jit(solution)/shard_map/all_gather | solution.py:121
  77.9 0.0 copy-done.15
  77.9 0.2 fusion.11
  78.1 0.2 fusion.48
  78.3 1.0 %copy.34 = f32[1024,128]{0,1:T(8,128)} copy(f32[1024,128]{1,0:T(8,128)S(1)} %bitcast.47) | data formatting | bytes 1048576 | tf_op jit(solution)/shard_map/reshape | solution.py:28
  79.3 0.4 multiply_reduce_fusion.1
  79.7 0.3 multiply_convert_fusion.2
  80.1 0.0 copy-done.1
  80.1 0.4 fusion.55
  80.5 0.0 copy-done.5
  80.5 0.0 copy-start.4
  80.6 0.0 copy-start.10
  80.6 2.0 %fusion.53 = (f32[1024]{0:T(1024)S(1)}, f32[1024,128]{0,1:T(8,128)S(1)}) fusion(f32[1024,128]{0,1:T(8,128)} %copy.34, bf16[512,128]{1,0:T(8,128)(2,1)S(1)} %copy-done.12, f32[1024,512]{1,0:T(8,128)S(1)} %fusion.55, bf16[1024,128]{1,0:T(8,128)(2,1)S(1)} %multiply_convert_fusion.2, bf16[128,512]{1,0:T(8,128)(2,1)S(1)} %copy-done.13), kind=kOutput, calls=%fused_computation.87 | convolution fusion | flops 271842304 | bytes 3674112 | tf_op jit(solution)/shard_map/dot_general | solution.py:33
  82.5 0.1 multiply_reduce_fusion
  82.6 0.0 copy-done.4
  82.6 0.0 copy-done.10
  82.6 0.2 fusion.54
  82.9 0.1 fusion.18
  82.9 0.7 multiply_reduce_fusion.3
  (23 shorter events, 0.1 us)
Async XLA Ops:
  0.6 57.6 %copy-start = (bf16[384,384]{1,0:T(8,128)(2,1)S(1)}, bf16[384,384]{1,0:T(8,128)(2,1)}, u32[]{:S(2)}) copy-start(bf16[384,384]{1,0:T(8,128)(2,1)} %param.30) | copy-start | bytes 884740
  0.6 55.4 %copy-start.7 = (s32[128]{0:T(128)S(1)}, s32[128]{0:T(128)}, u32[]{:S(2)}) copy-start(s32[128]{0:T(128)} %param.22) | copy-start | bytes 1540
  0.7 55.4 %copy-start.8 = (s32[128]{0:T(128)S(1)}, s32[128]{0:T(128)}, u32[]{:S(2)}) copy-start(s32[128]{0:T(128)} %param.23) | copy-start | bytes 1540
  0.7 55.2 %copy-start.9 = (s32[128]{0:T(128)S(1)}, s32[128]{0:T(128)}, u32[]{:S(2)}) copy-start(s32[128]{0:T(128)} %param.24) | copy-start | bytes 1540
  0.7 55.4 %copy-start.3 = (bf16[66,128]{1,0:T(8,128)(2,1)S(1)}, bf16[66,128]{1,0:T(8,128)(2,1)}, u32[]{:S(2)}) copy-start(bf16[66,128]{1,0:T(8,128)(2,1)} %param.32) | copy-start | bytes 50692
  0.7 56.3 %copy-start.6 = (bf16[128,16]{0,1:T(8,128)(2,1)S(1)}, bf16[128,16]{0,1:T(8,128)(2,1)}, u32[]{:S(2)}) copy-start(bf16[128,16]{0,1:T(8,128)(2,1)} %param.31) | copy-start | bytes 12292
  0.7 55.4 %all-to-all-start = ((bf16[128,8,128]{2,1,0:T(8,128)(2,1)}), bf16[128,8,128]{2,1,0:T(8,128)(2,1)S(1)}, u32[]{:S(2)}, u32[]{:S(2)}) async-start(bf16[128,8,128]{2,1,0:T(8,128)(2,1)} %param.20), calls=%async_computation | async-start | bytes 524288 | tf_op jit(solution)/shard_map/all_to_all | solution.py:77
  11.1 47.1 %copy-start.2 = (bf16[8,384]{1,0:T(8,128)(2,1)S(1)}, bf16[8,384]{1,0:T(8,128)(2,1)}, u32[]{:S(2)}) copy-start(bf16[8,384]{1,0:T(8,128)(2,1)} %param.21) | copy-start | bytes 18436
  11.1 47.1 %copy-start.11 = (bf16[384,384]{1,0:T(8,128)(2,1)S(1)}, bf16[384,384]{1,0:T(8,128)(2,1)}, u32[]{:S(2)}) copy-start(bf16[384,384]{1,0:T(8,128)(2,1)} %param.29) | copy-start | bytes 884740
  36.0 22.9 %copy-start.14 = (bf16[384,128]{1,0:T(8,128)(2,1)S(1)}, bf16[384,128]{1,0:T(8,128)(2,1)}, u32[]{:S(2)}) copy-start(bf16[384,128]{1,0:T(8,128)(2,1)} %param.34) | copy-start | bytes 294916
  37.2 40.7 %copy-start.15 = (bf16[384,128]{1,0:T(8,128)(2,1)S(1)}, bf16[384,128]{1,0:T(8,128)(2,1)}, u32[]{:S(2)}) copy-start(bf16[384,128]{1,0:T(8,128)(2,1)} %param.33) | copy-start | bytes 294916
  58.7 21.8 %copy-start.5 = (bf16[8,384]{1,0:T(8,128)(2,1)}, bf16[8,384]{1,0:T(8,128)(2,1)S(1)}, u32[]{:S(2)}) copy-start(bf16[8,384]{1,0:T(8,128)(2,1)S(1)} %get-tuple-element.11) | copy-start | bytes 18436
  58.7 21.4 %copy-start.1 = (bf16[128,512]{1,0:T(8,128)(2,1)S(1)}, bf16[128,512]{1,0:T(8,128)(2,1)}, u32[]{:S(2)}) copy-start(bf16[128,512]{1,0:T(8,128)(2,1)} %param.36) | copy-start | bytes 393220
  79.3 1.2 %copy-start.12 = (bf16[512,128]{1,0:T(8,128)(2,1)S(1)}, bf16[512,128]{1,0:T(8,128)(2,1)}, u32[]{:S(2)}) copy-start(bf16[512,128]{1,0:T(8,128)(2,1)} %param.37) | copy-start | bytes 393220
  79.3 1.2 %copy-start.13 = (bf16[128,512]{1,0:T(8,128)(2,1)S(1)}, bf16[128,512]{1,0:T(8,128)(2,1)}, u32[]{:S(2)}) copy-start(bf16[128,512]{1,0:T(8,128)(2,1)} %param.35) | copy-start | bytes 393220
  80.5 2.1 %copy-start.4 = (bf16[128,64]{0,1:T(8,128)(2,1)S(1)}, bf16[128,64]{0,1:T(8,128)(2,1)}, u32[]{:S(2)}) copy-start(bf16[128,64]{0,1:T(8,128)(2,1)} %param.38) | copy-start | bytes 49156
  80.6 2.1 %copy-start.10 = (f32[64]{0:T(128)S(1)}, f32[64]{0:T(128)}, u32[]{:S(2)}) copy-start(f32[64]{0:T(128)} %param.39) | copy-start | bytes 772
where the time goes:
time: 84.1 us; the launch traced here: 83.6 us
  blocking collectives  58.6 us (70%)
  matrix products  8.32 us (10%)
  starting transfers between devices  7.53 us (9%)
  other arithmetic  5.09 us (6%)
  local copies, waits for them, and re-layouts  3.06 us (4%)
  between operations  0.98 us (1%)
    all_gather x1, blocking collectives, on_device(): value_part = lax.all_gather(values_local, 'rows', axis=0, tiled=True)  22.1 us
    all_gather x1, blocking collectives, on_device(): every_b = lax.all_gather(factor_b, 'rows', axis=0, tiled=True)  18.8 us
    all_gather x1, blocking collectives, on_device(): key_part = lax.all_gather(keys_local, 'rows', axis=0, tiled=True)  17.7 us
    all_to_all x1, starting transfers between devices, on_device(): lax.all_to_all(pair_repr, 'rows', split_axis=0, concat_axis=1, tiled=True)  7.53 us
    dot_general x1, matrix products, pair_tail(): jnp.dot(hidden, w_hidden_out, preferred_element_type=jnp.float32)  1.96 us
    reduce_sum x5, other arithmetic, norm_rows(): spread = jnp.mean(center * center, axis=-1, keepdims=True)  1.87 us
  transfers between devices with their start and end apart: 1, of which 0 were waited for; matrix products, arithmetic and copies ran while one was open for 10% of the time, Pallas kernels for 0%

commit v1 on v0

--- a/solution.py
+++ b/solution.py
@@ -74,7 +74,12 @@
     keys_local = jnp.dot(normed, w_key, preferred_element_type=jnp.float32).astype(jnp.bfloat16)
     values_local = jnp.dot(normed, w_value, preferred_element_type=jnp.float32).astype(jnp.bfloat16)
     gating = jax.nn.sigmoid(jnp.dot(normed, w_gate, preferred_element_type=jnp.float32))
-    pair_local = lax.all_to_all(pair_repr, "rows", split_axis=0, concat_axis=1, tiled=True)
+    pair_local = jnp.concatenate(
+        lax.all_to_all(
+            jnp.stack(jnp.split(pair_repr, lax.axis_size("rows"), axis=0)), "rows", 0, 0
+        ),
+        axis=1,
+    )
     pair_in = pair_local.astype(jnp.float32) + relative(
         res_local, chain_local, residue_index, chain_index, rel_table
     )

time: 84.1 us -> 106 us (1.26); the launches traced: 83.6 us -> 104 us
  local copies, waits for them, and re-layouts: 3.06 us -> 24.2 us
    unnamed x32 -> x49, local copies, waits for them, and re-layouts: 0.08 us -> 19.9 us
    another operation x0 -> x1, local copies, waits for them, and re-layouts: none -> 1.32 us  [on_device(): jnp.stack(jnp.split(pair_repr, lax.axis_size('rows'), axis=0))]
  transfers between devices with their start and end apart: 1 -> 1, of which waited for: 0 -> 0; matrix products, arithmetic and copies ran while one was open for 10% -> 7% of each run, Pallas kernels for 0% -> 0%
where the time goes in v1:
time: 106 us; the launch traced here: 104 us
  blocking collectives  58.8 us (55%)
  local copies, waits for them, and re-layouts  24.2 us (23%)
  matrix products  8.32 us (8%)
  starting transfers between devices  7.39 us (7%)
  other arithmetic  4.39 us (4%)
    all_gather x1, blocking collectives, on_device(): value_part = lax.all_gather(values_local, 'rows', axis=0, tiled=True)  22.1 us
    unnamed x49, local copies, waits for them, and re-layouts  19.9 us
    all_gather x1, blocking collectives, on_device(): every_b = lax.all_gather(factor_b, 'rows', axis=0, tiled=True)  18.8 us
    all_gather x1, blocking collectives, on_device(): key_part = lax.all_gather(keys_local, 'rows', axis=0, tiled=True)  17.8 us
    all_to_all x1, starting transfers between devices, on_device(): lax.all_to_all(jnp.stack(jnp.split(pair_repr, lax.axis_size('rows'), axis...  7.39 us
  transfers between devices with their start and end apart: 1, of which 0 were waited for; matrix products, arithmetic and copies ran while one was open for 7% of the time, Pallas kernels for 0%

profile of v1, /device:TPU:0, one launch (start us, length us, event | category | flops | bytes accessed | tf_op | source)
XLA Modules:
  0.0 104.1 jit_solution(6689962023301109946)
XLA Ops:
  0.6 0.0 copy-start
  0.6 0.0 copy-start.7
  0.7 0.0 copy-start.8
  0.7 0.0 copy-start.16
  0.7 0.0 copy-start.9
  0.7 1.4 %constant_dynamic-update-slice_fusion.15 = bf16[16,8,8,128]{3,2,1,0:T(8,128)(2,1)} fusion(bf16[128,8,128]{2,1,0:T(8,128)(2,1)} %param.20), kind=kLoop, calls=%fused_computation.62 | loop fusion | bytes 32768
  2.1 1.3 %constant_dynamic-update-slice_fusion.14 = bf16[16,8,8,128]{3,2,1,0:T(8,128)(2,1)} fusion(bf16[16,8,8,128]{3,2,1,0:T(8,128)(2,1)} %constant_dynamic-update-slice_fusion.15, bf16[128,8,128]{2,1,0:T(8,128)(2,1)} %param.20), kind=kLoop, calls=%fused_computation.61 | loop fusion | bytes 32768
  3.4 1.3 %constant_dynamic-update-slice_fusion.13 = bf16[16,8,8,128]{3,2,1,0:T(8,128)(2,1)} fusion(bf16[16,8,8,128]{3,2,1,0:T(8,128)(2,1)} %constant_dynamic-update-slice_fusion.14, bf16[128,8,128]{2,1,0:T(8,128)(2,1)} %param.20), kind=kLoop, calls=%fused_computation.60 | loop fusion | bytes 32768
  4.7 1.3 %constant_dynamic-update-slice_fusion.12 = bf16[16,8,8,128]{3,2,1,0:T(8,128)(2,1)} fusion(bf16[16,8,8,128]{3,2,1,0:T(8,128)(2,1)} %constant_dynamic-update-slice_fusion.13, bf16[128,8,128]{2,1,0:T(8,128)(2,1)} %param.20), kind=kLoop, calls=%fused_computation.59 | loop fusion | bytes 32768
  6.1 1.3 %constant_dynamic-update-slice_fusion.11 = bf16[16,8,8,128]{3,2,1,0:T(8,128)(2,1)} fusion(bf16[16,8,8,128]{3,2,1,0:T(8,128)(2,1)} %constant_dynamic-update-slice_fusion.12, bf16[128,8,128]{2,1,0:T(8,128)(2,1)} %param.20), kind=kLoop, calls=%fused_computation.58 | loop fusion | bytes 32768
  7.4 1.3 %constant_dynamic-update-slice_fusion.10 = bf16[16,8,8,128]{3,2,1,0:T(8,128)(2,1)} fusion(bf16[16,8,8,128]{3,2,1,0:T(8,128)(2,1)} %constant_dynamic-update-slice_fusion.11, bf16[128,8,128]{2,1,0:T(8,128)(2,1)} %param.20), kind=kLoop, calls=%fused_computation.57 | loop fusion | bytes 32768
  8.7 1.3 %constant_dynamic-update-slice_fusion.9 = bf16[16,8,8,128]{3,2,1,0:T(8,128)(2,1)} fusion(bf16[16,8,8,128]{3,2,1,0:T(8,128)(2,1)} %constant_dynamic-update-slice_fusion.10, bf16[128,8,128]{2,1,0:T(8,128)(2,1)} %param.20), kind=kLoop, calls=%fused_computation.56 | loop fusion | bytes 32768
  10.0 1.3 %constant_dynamic-update-slice_fusion.8 = bf16[16,8,8,128]{3,2,1,0:T(8,128)(2,1)} fusion(bf16[16,8,8,128]{3,2,1,0:T(8,128)(2,1)} %constant_dynamic-update-slice_fusion.9, bf16[128,8,128]{2,1,0:T(8,128)(2,1)} %param.20), kind=kLoop, calls=%fused_computation.55 | loop fusion | bytes 32768
  11.3 1.3 %constant_dynamic-update-slice_fusion.7 = bf16[16,8,8,128]{3,2,1,0:T(8,128)(2,1)} fusion(bf16[16,8,8,128]{3,2,1,0:T(8,128)(2,1)} %constant_dynamic-update-slice_fusion.8, bf16[128,8,128]{2,1,0:T(8,128)(2,1)} %param.20), kind=kLoop, calls=%fused_computation.54 | loop fusion | bytes 32768
  12.6 1.3 %constant_dynamic-update-slice_fusion.6 = bf16[16,8,8,128]{3,2,1,0:T(8,128)(2,1)} fusion(bf16[16,8,8,128]{3,2,1,0:T(8,128)(2,1)} %constant_dynamic-update-slice_fusion.7, bf16[128,8,128]{2,1,0:T(8,128)(2,1)} %param.20), kind=kLoop, calls=%fused_computation.53 | loop fusion | bytes 32768
  13.9 1.3 %constant_dynamic-update-slice_fusion.5 = bf16[16,8,8,128]{3,2,1,0:T(8,128)(2,1)} fusion(bf16[16,8,8,128]{3,2,1,0:T(8,128)(2,1)} %constant_dynamic-update-slice_fusion.6, bf16[128,8,128]{2,1,0:T(8,128)(2,1)} %param.20), kind=kLoop, calls=%fused_computation.52 | loop fusion | bytes 32768
  15.3 1.3 %constant_dynamic-update-slice_fusion.4 = bf16[16,8,8,128]{3,2,1,0:T(8,128)(2,1)} fusion(bf16[16,8,8,128]{3,2,1,0:T(8,128)(2,1)} %constant_dynamic-update-slice_fusion.5, bf16[128,8,128]{2,1,0:T(8,128)(2,1)} %param.20), kind=kLoop, calls=%fused_computation.51 | loop fusion | bytes 32768
  16.6 1.3 %constant_dynamic-update-slice_fusion.3 = bf16[16,8,8,128]{3,2,1,0:T(8,128)(2,1)} fusion(bf16[16,8,8,128]{3,2,1,0:T(8,128)(2,1)} %constant_dynamic-update-slice_fusion.4, bf16[128,8,128]{2,1,0:T(8,128)(2,1)} %param.20), kind=kLoop, calls=%fused_computation.50 | loop fusion | bytes 32768
  17.9 1.3 %constant_dynamic-update-slice_fusion.2 = bf16[16,8,8,128]{3,2,1,0:T(8,128)(2,1)} fusion(bf16[16,8,8,128]{3,2,1,0:T(8,128)(2,1)} %constant_dynamic-update-slice_fusion.3, bf16[128,8,128]{2,1,0:T(8,128)(2,1)} %param.20), kind=kLoop, calls=%fused_computation.49 | loop fusion | bytes 32768
  19.2 1.3 %constant_dynamic-update-slice_fusion.1 = bf16[16,8,8,128]{3,2,1,0:T(8,128)(2,1)} fusion(bf16[16,8,8,128]{3,2,1,0:T(8,128)(2,1)} %constant_dynamic-update-slice_fusion.2, bf16[128,8,128]{2,1,0:T(8,128)(2,1)} %param.20), kind=kLoop, calls=%fused_computation.48 | loop fusion | bytes 32768
  20.5 1.3 %constant_dynamic-update-slice_fusion = bf16[16,8,8,128]{3,2,1,0:T(8,128)(2,1)} fusion(bf16[16,8,8,128]{3,2,1,0:T(8,128)(2,1)} %constant_dynamic-update-slice_fusion.1, bf16[128,8,128]{2,1,0:T(8,128)(2,1)} %param.20), kind=kLoop, calls=%fused_computation.47 | loop fusion | bytes 32768 | tf_op jit(solution)/shard_map/stack | solution.py:79
  21.9 7.4 %all-to-all-start = ((bf16[16,8,8,128]{3,2,1,0:T(8,128)(2,1)}), bf16[16,8,8,128]{3,2,1,0:T(8,128)(2,1)S(1)}, u32[]{:S(2)}, u32[]{:S(2)}) async-start(bf16[16,8,8,128]{3,2,1,0:T(8,128)(2,1)} %constant_dynamic-update-slice_fusion), calls=%async_computation | async-start | bytes 524288 | tf_op jit(solution)/shard_map/all_to_all | solution.py:78
  29.3 0.8 convert_reduce_fusion
  30.1 0.9 fusion.30
  31.0 1.2 %convolution_convert_fusion = bf16[8,384]{1,0:T(8,128)(2,1)S(1)} fusion(bf16[384,384]{1,0:T(8,128)(2,1)} %param.28, bf16[8,384]{1,0:T(8,128)(2,1)} %param.21, f32[8]{0:T(128)S(1)} %add_rsqrt_fusion.3, f32[8]{0:T(128)S(1)} %broadcast_multiply_fusion.4), kind=kOutput, calls=%fused_computation.18 | convolution fusion | flops 2374656 | bytes 307264 | tf_op jit(solution)/shard_map/dot_general | solution.py:75
  32.2 22.1 %all_gather.10 = bf16[128,384]{1,0:T(8,128)(2,1)S(1)} all-gather(bf16[8,384]{1,0:T(8,128)(2,1)S(1)} %convolution_convert_fusion), channel_id=1, replica_groups=mesh['groups'=2,'rows'=16] {'rows'}, dimensions={0}, use_global_device_ids=true | all-gather | bytes 104448 | tf_op jit(solution)/shard_map/all_gather | solution.py:95
  54.3 0.1 copy.32
  54.4 0.7 dynamic_slice.11
  55.1 0.7 dynamic_slice.10
  55.9 1.2 %convolution_convert_fusion.1 = bf16[8,384]{1,0:T(8,128)(2,1)S(1)} fusion(bf16[384,384]{1,0:T(8,128)(2,1)} %param.27, bf16[8,384]{1,0:T(8,128)(2,1)} %param.21, f32[8]{0:T(128)S(1)} %add_rsqrt_fusion.3, f32[8]{0:T(128)S(1)} %broadcast_multiply_fusion.4), kind=kOutput, calls=%fused_computation.19 | convolution fusion | flops 2374656 | bytes 307264 | tf_op jit(solution)/shard_map/dot_general | solution.py:74
  57.0 1.2 %convolution_convert_fusion.2 = bf16[8,384]{1,0:T(8,128)(2,1)S(1)} fusion(bf16[384,384]{1,0:T(8,128)(2,1)} %param.26, bf16[8,384]{1,0:T(8,128)(2,1)} %param.21, f32[8]{0:T(128)S(1)} %add_rsqrt_fusion.3, f32[8]{0:T(128)S(1)} %broadcast_multiply_fusion.4), kind=kOutput, calls=%fused_computation.20 | convolution fusion | flops 2374656 | bytes 307264 | tf_op jit(solution)/shard_map/dot_general | solution.py:73
  58.3 17.8 %all_gather.9 = bf16[128,384]{1,0:T(8,128)(2,1)S(1)} all-gather(bf16[8,384]{1,0:T(8,128)(2,1)S(1)} %convolution_convert_fusion.1), channel_id=1, replica_groups=mesh['groups'=2,'rows'=16] {'rows'}, dimensions={0}, use_global_device_ids=true | all-gather | bytes 104448 | tf_op jit(solution)/shard_map/all_gather | solution.py:94
  76.1 0.1 copy.28
  76.2 0.1 reshape.245
  76.3 0.1 dynamic_slice.9
  76.4 0.1 fusion.37
  76.5 0.1 add_select_fusion
  76.6 0.0 all-to-all-done
  76.6 0.4 fusion.49
  77.0 0.4 multiply_reduce_fusion.2
  77.4 0.5 fusion.13
  77.9 0.2 fusion.50
  78.1 0.2 fusion.20
  78.3 0.2 fusion.2
  78.6 0.1 reshape.248
  78.7 0.5 convert_reduce_fusion.1
  79.2 0.0 copy-start.5
  79.2 0.0 copy-start.1
  79.2 0.2 fusion.32
  79.4 0.2 convolution_convert_fusion.3
  79.6 18.8 %all_gather.11 = bf16[128,128]{1,0:T(8,128)(2,1)S(1)} all-gather(bf16[8,128]{1,0:T(8,128)(2,1)S(1)} %convolution_convert_fusion.3), channel_id=1, replica_groups=mesh['groups'=2,'rows'=16] {'rows'}, dimensions={0}, use_global_device_ids=true | all-gather | bytes 34816 | tf_op jit(solution)/shard_map/all_gather | solution.py:126
  98.4 0.2 fusion.11
  98.6 0.2 fusion.48
  98.8 1.0 copy.34
  99.8 0.4 multiply_reduce_fusion.1
  100.2 0.3 multiply_convert_fusion.2
  100.6 0.4 fusion.55
  101.0 0.0 copy-start.4
  101.0 0.0 copy-start.10
  101.1 2.0 %fusion.53 = (f32[1024]{0:T(1024)S(1)}, f32[1024,128]{0,1:T(8,128)S(1)}) fusion(f32[1024,128]{0,1:T(8,128)} %copy.34, bf16[512,128]{1,0:T(8,128)(2,1)S(1)} %copy-done.12, f32[1024,512]{1,0:T(8,128)S(1)} %fusion.55, bf16[1024,128]{1,0:T(8,128)(2,1)S(1)} %multiply_convert_fusion.2, bf16[128,512]{1,0:T(8,128)(2,1)S(1)} %copy-done.13), kind=kOutput, calls=%fused_computation.104 | convolution fusion | flops 271842304 | bytes 3674112 | tf_op jit(solution)/shard_map/dot_general | solution.py:33
  103.0 0.1 multiply_reduce_fusion
  103.1 0.2 fusion.54
  103.3 0.1 fusion.18
  103.4 0.7 multiply_reduce_fusion.3
  (41 shorter events, 0.2 us)
Async XLA Ops:
  0.6 78.0 %copy-start = (bf16[384,384]{1,0:T(8,128)(2,1)S(1)}, bf16[384,384]{1,0:T(8,128)(2,1)}, u32[]{:S(2)}) copy-start(bf16[384,384]{1,0:T(8,128)(2,1)} %param.30) | copy-start | bytes 884740
  0.6 75.9 %copy-start.7 = (s32[128]{0:T(128)S(1)}, s32[128]{0:T(128)}, u32[]{:S(2)}) copy-start(s32[128]{0:T(128)} %param.22) | copy-start | bytes 1540
  0.7 75.8 %copy-start.8 = (s32[128]{0:T(128)S(1)}, s32[128]{0:T(128)}, u32[]{:S(2)}) copy-start(s32[128]{0:T(128)} %param.23) | copy-start | bytes 1540
  0.7 57.6 %copy-start.16 = (s32[128]{0:T(128)S(1)}, s32[128]{0:T(128)}, u32[]{:S(2)}) copy-start(s32[128]{0:T(128)} %param.25) | copy-start | bytes 1540
  0.7 75.7 %copy-start.9 = (s32[128]{0:T(128)S(1)}, s32[128]{0:T(128)}, u32[]{:S(2)}) copy-start(s32[128]{0:T(128)} %param.24) | copy-start | bytes 1540
  0.7 75.9 %copy-start.3 = (bf16[66,128]{1,0:T(8,128)(2,1)S(1)}, bf16[66,128]{1,0:T(8,128)(2,1)}, u32[]{:S(2)}) copy-start(bf16[66,128]{1,0:T(8,128)(2,1)} %param.32) | copy-start | bytes 50692
  0.7 76.7 %copy-start.6 = (bf16[128,16]{0,1:T(8,128)(2,1)S(1)}, bf16[128,16]{0,1:T(8,128)(2,1)}, u32[]{:S(2)}) copy-start(bf16[128,16]{0,1:T(8,128)(2,1)} %param.31) | copy-start | bytes 12292
  21.9 54.7 %all-to-all-start = ((bf16[16,8,8,128]{3,2,1,0:T(8,128)(2,1)}), bf16[16,8,8,128]{3,2,1,0:T(8,128)(2,1)S(1)}, u32[]{:S(2)}, u32[]{:S(2)}) async-start(bf16[16,8,8,128]{3,2,1,0:T(8,128)(2,1)} %constant_dynamic-update-slice_fusion), calls=%async_computation | async-start | bytes 524288 | tf_op jit(solution)/shard_map/all_to_all | solution.py:78
  32.1 46.5 %copy-start.2 = (bf16[8,384]{1,0:T(8,128)(2,1)S(1)}, bf16[8,384]{1,0:T(8,128)(2,1)}, u32[]{:S(2)}) copy-start(bf16[8,384]{1,0:T(8,128)(2,1)} %param.21) | copy-start | bytes 18436
  32.1 46.5 %copy-start.11 = (bf16[384,384]{1,0:T(8,128)(2,1)S(1)}, bf16[384,384]{1,0:T(8,128)(2,1)}, u32[]{:S(2)}) copy-start(bf16[384,384]{1,0:T(8,128)(2,1)} %param.29) | copy-start | bytes 884740
  57.0 22.4 %copy-start.14 = (bf16[384,128]{1,0:T(8,128)(2,1)S(1)}, bf16[384,128]{1,0:T(8,128)(2,1)}, u32[]{:S(2)}) copy-start(bf16[384,128]{1,0:T(8,128)(2,1)} %param.34) | copy-start | bytes 294916
  58.2 40.2 %copy-start.15 = (bf16[384,128]{1,0:T(8,128)(2,1)S(1)}, bf16[384,128]{1,0:T(8,128)(2,1)}, u32[]{:S(2)}) copy-start(bf16[384,128]{1,0:T(8,128)(2,1)} %param.33) | copy-start | bytes 294916
  79.2 21.8 %copy-start.5 = (bf16[8,384]{1,0:T(8,128)(2,1)}, bf16[8,384]{1,0:T(8,128)(2,1)S(1)}, u32[]{:S(2)}) copy-start(bf16[8,384]{1,0:T(8,128)(2,1)S(1)} %get-tuple-element.11) | copy-start | bytes 18436
  79.2 21.4 %copy-start.1 = (bf16[128,512]{1,0:T(8,128)(2,1)S(1)}, bf16[128,512]{1,0:T(8,128)(2,1)}, u32[]{:S(2)}) copy-start(bf16[128,512]{1,0:T(8,128)(2,1)} %param.36) | copy-start | bytes 393220
  99.8 1.2 %copy-start.12 = (bf16[512,128]{1,0:T(8,128)(2,1)S(1)}, bf16[512,128]{1,0:T(8,128)(2,1)}, u32[]{:S(2)}) copy-start(bf16[512,128]{1,0:T(8,128)(2,1)} %param.37) | copy-start | bytes 393220
  99.8 1.2 %copy-start.13 = (bf16[128,512]{1,0:T(8,128)(2,1)S(1)}, bf16[128,512]{1,0:T(8,128)(2,1)}, u32[]{:S(2)}) copy-start(bf16[128,512]{1,0:T(8,128)(2,1)} %param.35) | copy-start | bytes 393220
  101.0 2.1 %copy-start.4 = (bf16[128,64]{0,1:T(8,128)(2,1)S(1)}, bf16[128,64]{0,1:T(8,128)(2,1)}, u32[]{:S(2)}) copy-start(bf16[128,64]{0,1:T(8,128)(2,1)} %param.38) | copy-start | bytes 49156
  101.0 2.1 %copy-start.10 = (f32[64]{0:T(128)S(1)}, f32[64]{0:T(128)}, u32[]{:S(2)}) copy-start(f32[64]{0:T(128)} %param.39) | copy-start | bytes 772
